TPU v7x, 512 devices: a whole 4x8x8 slice. The times are simulated.
512 devices in a mesh: atoms: 32 (over z, x), modes: 16 (over y, core).
Axes of the slice: x: 4, y: 8, z: 8, core: 2. Of those that a mesh axis runs over, the one named last changes fastest.
Arguments:
- subspace: float32 [768, 65536], P('modes', 'atoms'), may hold values from -100 to 100
- applied: float32 [768, 65536], P('modes', 'atoms'), may hold values from -300 to 300
Outputs:
- ortho_basis: float32 [768, 65536], P('modes', 'atoms')
- projected: float32 [768, 768], P('modes')
All inputs are finite; a program needn't handle non-finite values.
Results may differ from a plain program's by a relative error of at most 0.00025.
Values sent between devices are 32-bit elements; how exact they have to be, the bound alone decides.
A program may use at most 64 MiB of HBM per device.

v0:
```python
import jax
import jax.numpy as jnp
from jax import lax
from jax.experimental import pallas as pl
from jax.experimental.pallas import tpu as pltpu
from jax.sharding import PartitionSpec as P


def in_blocks(value, dim, count):
    lengths = value.shape
    tiles = value.reshape(*lengths[:dim], count, lengths[dim] // count, *lengths[dim + 1 :])
    return jnp.moveaxis(tiles, dim, 0)


def sum_at_owner(value, axis, dim):
    count = lax.axis_size(axis)
    tiles = lax.all_to_all(in_blocks(value, dim, count), axis, 0, 0, tiled=True)
    return jnp.sum(tiles, axis=0)


def rows_for(lines, count):
    spare = -len(lines) % count
    return jnp.pad(lines, [(0, spare)] + [(0, 0)] * (lines.ndim - 1))


def copy_for_each(value, axis):
    count = lax.axis_size(axis)
    return lax.all_to_all(
        jnp.broadcast_to(value[None], (count, *value.shape)), axis, 0, 0, tiled=True
    )


def laid_out(tiles, dim):
    lengths = list(tiles.shape[1:])
    lengths[dim] *= tiles.shape[0]
    return jnp.moveaxis(tiles, 0, dim).reshape(lengths)


def collect(value, axis, dim):
    tiles = copy_for_each(value, axis)
    return laid_out(tiles, dim)


def nested_sum(value, axes):
    own = sum_at_owner(rows_for(value, lax.axis_size(axes)), axes, 0)
    whole = collect(own, axes, 0)
    return whole[: len(value)].reshape(value.shape)


def together(arrays, axis):
    ends = [0]
    for a in arrays:
        ends.append(ends[-1] + a.size)
    running = nested_sum(jnp.concatenate([a.ravel() for a in arrays]), axis)
    return tuple((running[b:e].reshape(a.shape) for a, b, e in zip(arrays, ends, ends[1:])))


def sent_together(arrays, axis, dim, along):
    both = jnp.concatenate(arrays, axis=along)
    out, at, gathered = (lax.all_gather(both, axis, axis=dim, tiled=True), 0, [])
    for a in arrays:
        gathered.append(lax.slice_in_dim(out, at, at + a.shape[along], axis=along))
        at += a.shape[along]
    return tuple(gathered)


def contract_cols(left, right):
    return lax.dot_general(
        left,
        right,
        (((1,), (1,)), ((), ())),
        precision=lax.Precision.HIGHEST,
        preferred_element_type=jnp.float32,
    )


def matmul(left, right):
    return jnp.dot(left, right, precision=lax.Precision.HIGHEST, preferred_element_type=jnp.float32)


B = 128
HI = lax.Precision.HIGHEST


def lane_bcast(v, j):
    return jnp.broadcast_to(v[:, j : j + 1], v.shape)


def row_bcast(v, j):
    return jnp.broadcast_to(v[j : j + 1, :], v.shape)


def factor_block(d_ref, m_ref):
    lane = lax.broadcasted_iota(jnp.int32, (8, B), 1)
    sub = lax.broadcasted_iota(jnp.int32, (8, B), 0)
    for s in range(B // 8):
        m_ref[8 * s : 8 * s + 8, :] = jnp.where(lane == sub + 8 * s, 1.0, 0.0)
    groups = B // 8
    for s in range(groups):
        r0 = 8 * s
        d = d_ref[r0 : r0 + 8, :]
        m = m_ref[r0 : r0 + 8, :]
        col = [lane_bcast(d, r0 + k) for k in range(8)]
        last = s == groups - 1
        if not last:
            nd = d_ref[r0 + 8 : r0 + 16, :]
            nm = m_ref[r0 + 8 : r0 + 16, :]
            ncol = [lane_bcast(nd, r0 + k) for k in range(8)]
        scale = None
        for j in range(8):
            pivot = row_bcast(col[j], j)
            inv = 1.0 / pivot
            root = lax.rsqrt(pivot)
            scale = root if scale is None else jnp.where(sub >= j, root, scale)
            dj = row_bcast(d, j) * inv
            mj = row_bcast(m, j) * inv
            for k in range(j + 1, 8):
                f = row_bcast(col[k], j) * inv
                if j < 7:
                    col[k] = col[k] - col[j] * f
                if not last:
                    ncol[k] = ncol[k] - ncol[j] * f
            below = jnp.where(sub > j, col[j], 0.0)
            if j < 7:
                d = d - below * dj
                m = m - below * mj
            if not last:
                nd = nd - ncol[j] * dj
                nm = nm - ncol[j] * mj
        d = d * scale
        m = m * scale
        m_ref[r0 : r0 + 8, :] = m
        if not last:
            d_ref[r0 + 8 : r0 + 16, :] = nd
            m_ref[r0 + 8 : r0 + 16, :] = nm
        if s < groups - 2:
            t = d.T
            drow = [row_bcast(d, j) for j in range(8)]
            mrow = [row_bcast(m, j) for j in range(8)]
            for g in range(s + 2, groups):
                tg = t[8 * g : 8 * g + 8, :]
                xd = d_ref[8 * g : 8 * g + 8, :]
                xm = m_ref[8 * g : 8 * g + 8, :]
                for j in range(8):
                    c = jnp.broadcast_to(tg[:, j : j + 1], (8, B))
                    xd = xd - c * drow[j]
                    xm = xm - c * mrow[j]
                d_ref[8 * g : 8 * g + 8, :] = xd
                m_ref[8 * g : 8 * g + 8, :] = xm


def dot(a, b, dims):
    return lax.dot_general(a, b, (dims, ((), ())), precision=HI, preferred_element_type=jnp.float32)


def invert_lower(z_ref, d_ref, m_ref):
    n = z_ref.shape[0]
    steps = n // B

    @pl.loop(0, steps)
    def _(k):
        k0 = pl.multiple_of(k * B, B)
        d_ref[...] = z_ref[pl.ds(k0, B), pl.ds(k0, B)]
        factor_block(d_ref, m_ref)
        for kk in range(steps):
            @pl.when(k == kk)
            def _():
                lo, hi = kk * B, (kk + 1) * B
                m = m_ref[...]
                if kk:
                    z_ref[lo:hi, :lo] = dot(m, z_ref[lo:hi, :lo], ((1,), (0,)))
                z_ref[lo:hi, lo:hi] = m
                if hi < n:
                    r = dot(m, z_ref[lo:hi, hi:], ((1,), (0,)))
                    z_ref[hi:, lo:hi] = jnp.zeros((n - hi, B), jnp.float32)
                    z_ref[lo:hi, hi:] = jnp.zeros((B, n - hi), jnp.float32)
                    rt = r.T
                    z_ref[hi:, :hi] -= dot(rt, z_ref[lo:hi, :hi], ((1,), (0,)))
                    z_ref[hi:, hi:] -= dot(rt, r, ((1,), (0,)))


def chol_kernel(g_ref, z_ref, d_ref, m_ref):
    z_ref[...] = g_ref[...]
    invert_lower(z_ref, d_ref, m_ref)


def inverse_factor(gram):
    n = gram.shape[0]
    vm = pl.BlockSpec(memory_space=pltpu.VMEM)
    return pl.pallas_call(
        chol_kernel,
        out_shape=jax.ShapeDtypeStruct((n, n), jnp.float32),
        in_specs=[vm], out_specs=vm,
        scratch_shapes=[pltpu.VMEM((B, B), jnp.float32), pltpu.VMEM((B, B), jnp.float32)],
        compiler_params=pltpu.CompilerParams(vmem_limit_bytes=48 * 2**20),
        name="inverse_factor",
    )(gram)


def per_device(subspace, applied):
    mode_width = subspace.shape[0]
    row_total = subspace.shape[1] * lax.axis_size("atoms")
    mode_start = lax.axis_index("modes") * mode_width
    full_modes = lax.all_gather(subspace, "modes", axis=0, tiled=True)
    gram_part = contract_cols(subspace, full_modes) / row_total
    crosst_part = contract_cols(applied, full_modes) / row_total
    gram_rows, crosst_rows = together((gram_part, crosst_part), "atoms")
    gram_full, crosst_full = sent_together((gram_rows, crosst_rows), "modes", 0, 1)
    inv_lower = inverse_factor(gram_full)
    inv_upper = inv_lower.T
    lower_rows = lax.dynamic_slice_in_dim(inv_lower, mode_start, mode_width, 0)
    ortho_basis = matmul(lower_rows, full_modes)
    projected = matmul(matmul(lower_rows, crosst_full.T), inv_upper)
    return (ortho_basis, projected)


def solution(mesh):
    return jax.shard_map(
        per_device,
        mesh=mesh,
        in_specs=(P("modes", "atoms"), P("modes", "atoms")),
        out_specs=(P("modes", "atoms"), P("modes", None)),
        check_vma=False,
    )
```

profile of v0, /device:TPU:1, one launch (start us, length us, event | category | flops | bytes accessed | tf_op | source)
XLA Modules:
  0.0 220.0 jit_solution(5285103771271809216)
XLA Ops:
  7.2 0.0 copy-start
  7.2 0.0 all-gather.3.cloned.1.call-start
  7.2 0.7 all-gather.3.cloned.1.call-update
  7.9 0.0 all-gather.5.cloned.1.call-start
  8.0 56.6 %all-gather.3.cloned.1.call-done = f32[768,2048]{1,0:T(8,128)} async-done(((f32[48,2048]{1,0:T(8,128)}), f32[768,2048]{1,0:T(8,128)}) %all-gather.3.cloned.1.call-update) | async-done | bytes 6291472 | tf_op jit(solution)/shard_map/all_gather | solution.py:204
  64.6 8.8 %convolution_multiply_fusion.1 = f32[48,768]{1,0:T(8,128)S(1)} fusion(f32[48,2048]{1,0:T(8,128)} %param.2, f32[768,2048]{1,0:T(8,128)} %all-gather.3.cloned.1.call-done), kind=kOutput, calls=%fused_computation.3 | convolution fusion | flops 906006528 | bytes 6832128 | tf_op jit(solution)/shard_map/dot_general | solution.py:68
  73.4 0.0 copy-done
  73.4 8.6 %convolution_multiply_fusion = f32[48,768]{1,0:T(8,128)S(1)} fusion(f32[48,2048]{1,0:T(8,128)S(1)} %copy-done, f32[768,2048]{1,0:T(8,128)} %all-gather.3.cloned.1.call-done), kind=kOutput, calls=%fused_computation.2 | convolution fusion | flops 906006528 | bytes 6832128 | tf_op jit(solution)/shard_map/dot_general | solution.py:68
  82.1 0.2 all_to_all.10
  82.4 22.0 %all_to_all.15 = f32[32,1,2304]{2,1,0:T(1,128)S(1)} all-to-all(f32[32,1,2304]{2,1,0:T(1,128)S(1)} %all_to_all.10), channel_id=1, replica_groups=mesh['atoms'=32,'modes'=16] {'atoms'}, dimensions={0} | all-to-all | bytes 589824 | tf_op jit(solution)/shard_map/all_to_all | solution.py:17
  104.3 0.2 reduce_sum.9
  104.5 0.2 broadcast_in_dim.2
  104.7 15.3 %all_to_all.16 = f32[32,1,2304]{2,1,0:T(1,128)S(1)} all-to-all(f32[32,1,2304]{2,1,0:T(1,128)S(1)} %broadcast_in_dim.2), channel_id=1, replica_groups=mesh['atoms'=32,'modes'=16] {'atoms'}, dimensions={0} | all-to-all | bytes 589824 | tf_op jit(solution)/shard_map/all_to_all | solution.py:28
  119.9 0.7 slice_reduce_fusion.1
  120.7 0.7 pad_maximum_fusion.1
  121.5 0.0 all-gather.5.cloned.1.call-update
  121.5 40.6 %all-gather.5.cloned.1.call-done = f32[768,1536]{1,0:T(8,128)} async-done(((f32[48,1536]{1,0:T(8,128)}), f32[768,1536]{1,0:T(8,128)}) %all-gather.5.cloned.1.call-update) | async-done | bytes 4718608 | tf_op jit(solution)/shard_map/all_gather | solution.py:60
  162.1 0.0 copy-start.1
  162.1 0.0 slice-start
  162.1 2.0 slice.22.g_ref
  164.1 0.0 slice-start.1
  164.1 39.2 %inverse_factor.1 = f32[768,768]{1,0:T(8,128)S(1)} custom-call(f32[768,768]{1,0:T(8,128)S(1)} %slice.22.g_ref), custom_call_target="tpu_custom_call" | custom-call | tf_op jit(solution)/shard_map/inverse_factor/pallas_call | solution.py:190
  203.3 0.0 copy-done.1
  203.3 2.3 %fusion = f32[48,768]{1,0:T(8,128)S(1)} fusion(f32[768,1536]{1,0:T(8,128)S(1)} %copy-done.1, f32[768,768]{1,0:T(8,128)S(1)} %inverse_factor.1, s32[]{:T(128)S(6)} %select_n.3), kind=kOutput, calls=%fused_computation | convolution fusion | flops 339738624 | bytes 2654212 | tf_op jit(solution)/shard_map/dot_general | solution.py:78
  205.6 3.0 %fusion.7 = f32[48,768]{1,0:T(8,128)} fusion(f32[48,768]{1,0:T(8,128)S(1)} %fusion, f32[768,768]{1,0:T(8,128)S(1)} %inverse_factor.1), kind=kOutput, calls=%fused_computation.13 | convolution fusion | flops 339738624 | bytes 2654208 | tf_op jit(solution)/shard_map/dot_general | solution.py:78
  208.6 0.0 slice-done
  208.6 0.0 slice-done.1
  208.6 4.6 %fusion.3 = f32[48,2048]{1,0:T(8,128)} fusion(f32[768,2048]{1,0:T(8,128)S(1)} %bitcast.8, f32[768,768]{1,0:T(8,128)S(1)} %inverse_factor.1, s32[]{:T(128)S(6)} %select_n.3), kind=kOutput, calls=%fused_computation.9 | convolution fusion | flops 905969664 | bytes 6832132 | tf_op jit(solution)/shard_map/dot_general | solution.py:78
  (6 shorter events, 0.2 us)
Async XLA Ops:
  7.2 66.2 %copy-start = (f32[48,2048]{1,0:T(8,128)S(1)}, f32[48,2048]{1,0:T(8,128)}, u32[]{:S(2)}) copy-start(f32[48,2048]{1,0:T(8,128)} %param.3) | copy-start | bytes 1179652
  7.2 57.4 %all-gather.3.cloned.1.call-start = ((), (), s32[]{:S(2)}) async-start(), calls=%async_computation.2 | async-start | bytes 6684672 | tf_op jit(solution)/shard_map/all_gather | solution.py:204
  7.9 154.2 %all-gather.5.cloned.1.call-start = ((), (), s32[]{:S(2)}) async-start(), calls=%async_computation.3 | async-start | bytes 5013504 | tf_op jit(solution)/shard_map/all_gather | solution.py:60
  162.1 41.2 %copy-start.1 = (f32[768,1536]{1,0:T(8,128)S(1)}, f32[768,1536]{1,0:T(8,128)}, u32[]{:S(2)}) copy-start(f32[768,1536]{1,0:T(8,128)} %all-gather.5.cloned.1.call-done) | copy-start | bytes 14155780
  162.1 46.5 %slice-start = ((s8[6291456]{0:T(1024)(128)(4,1)}), s8[4194304]{0:T(1024)(128)(4,1)S(1)}, s32[]{:S(2)}) async-start(s8[6291456]{0:T(1024)(128)(4,1)} %bitcast.7), calls=%async_computation.4 | async-start | bytes 8388608
  164.1 44.5 %slice-start.1 = ((s8[6291456]{0:T(1024)(128)(4,1)}), s8[2097152]{0:T(1024)(128)(4,1)S(1)}, s32[]{:S(2)}) async-start(s8[6291456]{0:T(1024)(128)(4,1)} %bitcast.7), calls=%async_computation.5 | async-start | bytes 4194304
Sparse Core Ops, SparseCore 0:
  10.1 54.4 all-gather.2
  121.6 40.4 all-gather.4
where the time goes:
time: 220 us
  waiting for transfers between devices  97.9 us (44%)
  Pallas kernels  39.2 us (18%)
  blocking collectives  37.2 us (17%)
  matrix products  27.2 us (12%)
  between operations  14.2 us (6%)
  local copies, waits for them, and re-layouts  3.24 us (1%)
    all_gather x1, waiting for transfers between devices, per_device(): full_modes = lax.all_gather(subspace, 'modes', axis=0, tiled=True)  56.6 us
    all_gather x1, waiting for transfers between devices, sent_together(): lax.all_gather(both, axis, axis=dim, tiled=True)  40.6 us
    pallas_call x1, Pallas kernels, inverse_factor(): pl.pallas_call(chol_kernel, out_shape=jax.ShapeDtypeStruct((n, n), jnp.fl...  39.2 us
    all_to_all x1, blocking collectives, sum_at_owner(): tiles = lax.all_to_all(in_blocks(value, dim, count), axis, 0, 0, tiled=True)  22 us
    dot_general x2, matrix products, contract_cols(): lax.dot_general(left, right, (((1,), (1,)), ((), ())), precision=lax.Prec...  17.4 us
    all_to_all x1, blocking collectives, copy_for_each(): lax.all_to_all(jnp.broadcast_to(value[None], (count, *value.shape)), axis...  15.3 us
    dot_general x3, matrix products, matmul(): jnp.dot(left, right, precision=lax.Precision.HIGHEST, preferred_element_t...  9.83 us
  transfers between devices with their start and end apart: 2, of which 2 were waited for; matrix products, arithmetic and copies ran while one was open for 0% of the time, Pallas kernels for 0%

commit v1 on v0

v1 whole, which is shorter than its diff:
```python
import functools

import jax
import jax.numpy as jnp
from jax import lax
from jax.experimental import pallas as pl
from jax.experimental.pallas import tpu as pltpu
from jax.sharding import PartitionSpec as P

MESH = pl.DeviceIdType.MESH
NX, NY, NZ = 4, 8, 8
UNITS = 12
UNIT_PLACES = [(i, p) for i in range(6) for p in range(i // 2 + 1)]
B = 128
HI = lax.Precision.HIGHEST


def lane_bcast(v, j):
    return jnp.broadcast_to(v[:, j : j + 1], v.shape)


def row_bcast(v, j):
    return jnp.broadcast_to(v[j : j + 1, :], v.shape)


def factor_block(d_ref, m_ref):
    lane = lax.broadcasted_iota(jnp.int32, (8, B), 1)
    sub = lax.broadcasted_iota(jnp.int32, (8, B), 0)
    for s in range(B // 8):
        m_ref[8 * s : 8 * s + 8, :] = jnp.where(lane == sub + 8 * s, 1.0, 0.0)
    groups = B // 8
    for s in range(groups):
        r0 = 8 * s
        d = d_ref[r0 : r0 + 8, :]
        m = m_ref[r0 : r0 + 8, :]
        col = [lane_bcast(d, r0 + k) for k in range(8)]
        last = s == groups - 1
        if not last:
            nd = d_ref[r0 + 8 : r0 + 16, :]
            nm = m_ref[r0 + 8 : r0 + 16, :]
            ncol = [lane_bcast(nd, r0 + k) for k in range(8)]
        scale = None
        for j in range(8):
            pivot = row_bcast(col[j], j)
            inv = 1.0 / pivot
            root = lax.rsqrt(pivot)
            scale = root if scale is None else jnp.where(sub >= j, root, scale)
            dj = row_bcast(d, j) * inv
            mj = row_bcast(m, j) * inv
            for k in range(j + 1, 8):
                f = row_bcast(col[k], j) * inv
                if j < 7:
                    col[k] = col[k] - col[j] * f
                if not last:
                    ncol[k] = ncol[k] - ncol[j] * f
            below = jnp.where(sub > j, col[j], 0.0)
            if j < 7:
                d = d - below * dj
                m = m - below * mj
            if not last:
                nd = nd - ncol[j] * dj
                nm = nm - ncol[j] * mj
        d = d * scale
        m = m * scale
        m_ref[r0 : r0 + 8, :] = m
        if not last:
            d_ref[r0 + 8 : r0 + 16, :] = nd
            m_ref[r0 + 8 : r0 + 16, :] = nm
        if s < groups - 2:
            t = d.T
            drow = [row_bcast(d, j) for j in range(8)]
            mrow = [row_bcast(m, j) for j in range(8)]
            for g in range(s + 2, groups):
                tg = t[8 * g : 8 * g + 8, :]
                xd = d_ref[8 * g : 8 * g + 8, :]
                xm = m_ref[8 * g : 8 * g + 8, :]
                for j in range(8):
                    c = jnp.broadcast_to(tg[:, j : j + 1], (8, B))
                    xd = xd - c * drow[j]
                    xm = xm - c * mrow[j]
                d_ref[8 * g : 8 * g + 8, :] = xd
                m_ref[8 * g : 8 * g + 8, :] = xm


def dot(a, b, dims):
    return lax.dot_general(a, b, (dims, ((), ())), precision=HI, preferred_element_type=jnp.float32)


def invert_lower(z_ref, d_ref, m_ref):
    n = z_ref.shape[0]
    steps = n // B

    @pl.loop(0, steps)
    def _(k):
        k0 = pl.multiple_of(k * B, B)
        d_ref[...] = z_ref[pl.ds(k0, B), pl.ds(k0, B)]
        factor_block(d_ref, m_ref)
        for kk in range(steps):
            @pl.when(k == kk)
            def _():
                lo, hi = kk * B, (kk + 1) * B
                m = m_ref[...]
                if kk:
                    z_ref[lo:hi, :lo] = dot(m, z_ref[lo:hi, :lo], ((1,), (0,)))
                z_ref[lo:hi, lo:hi] = m
                if hi < n:
                    r = dot(m, z_ref[hi:, lo:hi], ((1,), (1,)))
                    z_ref[hi:, lo:hi] = jnp.zeros((n - hi, B), jnp.float32)
                    z_ref[lo:hi, hi:] = jnp.zeros((B, n - hi), jnp.float32)
                    rt = r.T
                    z_ref[hi:, :hi] -= dot(rt, z_ref[lo:hi, :hi], ((1,), (0,)))
                    z_ref[hi:, hi:] -= dot(rt, r, ((1,), (0,)))


def copy_to(src, dst, send, recv, device):
    return pltpu.make_async_remote_copy(
        src_ref=src, dst_ref=dst, send_sem=send, recv_sem=recv, device_id=device, device_id_type=MESH
    )


def kernel(
    s_hbm, a_hbm, ortho_ref, proj_ref,
    s_all, a_own, g_part, g_x, g_z, g_all, c_part, c_x, c_z, c_all, z_ref, ct_ref, d_ref, m_ref,
    load_sem, ring_send, ring_recv, twin_send, twin_recv,
    gx_send, gx_recv, gz_send, gz_recv, gy_send, gy_recv, gg_send, gg_recv, gt_send, gt_recv,
    cx_send, cx_recv, cz_send, cz_recv, cy_send, cy_recv, cg_send, cg_recv, ct_send, ct_recv,
):
    atom, mode = lax.axis_index("atoms"), lax.axis_index("modes")
    z, x = atom // NX, atom % NX
    y, core = mode // 2, mode % 2
    rows = s_hbm.shape[0]
    half_rows = rows // 2
    total = s_hbm.shape[1] * NX * NZ
    wide = s_hbm.shape[1]

    def at_x(d):
        return (z * NX + (x + d) % NX, mode)

    def at_y(d):
        return (atom, ((y + d) % NY) * 2 + core)

    def at_z(d):
        return (((z + d) % NZ) * NX + x, mode)

    twin = (atom, y * 2 + (1 - core))

    own_s = pltpu.make_async_copy(
        s_hbm, s_all.at[pl.ds(pl.multiple_of(mode * rows, 8), rows), :], load_sem.at[0]
    )
    own_a = pltpu.make_async_copy(a_hbm, a_own, load_sem.at[1])
    own_s.start()
    own_a.start()
    barrier = pltpu.get_barrier_semaphore()
    peers = [at_x(d) for d in range(1, NX)] + [at_y(d) for d in range(1, NY)]
    peers += [at_z(d) for d in range(1, NZ)] + [twin]
    for peer in peers:
        pl.semaphore_signal(barrier, inc=1, device_id=peer, device_id_type=MESH)
    own_s.wait()
    pl.semaphore_wait(barrier, len(peers))

    pending = []

    def piece(back, which, q):
        start = (((y + NY - back) % NY) * 2 + which) * rows + q * half_rows
        return s_all.at[pl.ds(pl.multiple_of(start, 8), half_rows), :]

    def ring(way, hop, q):
        back = hop if way == 0 else (NY - hop) % NY
        ref = piece(back, core, q)
        return copy_to(
            ref, ref, ring_send.at[way, hop, q], ring_recv.at[way, hop, q], at_y(1 if way == 0 else NY - 1)
        )

    def ring_in(way, hop, q):
        back = hop + 1 if way == 0 else NY - hop - 1
        ref = piece(back, core, q)
        return copy_to(
            ref, ref, ring_send.at[way, hop, q], ring_recv.at[way, hop, q], at_y(1 if way == 0 else NY - 1)
        )

    def to_twin(back, q):
        ref = piece(back, core, q)
        return copy_to(ref, ref, twin_send.at[back, q], twin_recv.at[back, q], twin)

    def from_twin(back, q):
        ref = piece(back, 1 - core, q)
        return copy_to(ref, ref, twin_send.at[back, q], twin_recv.at[back, q], twin)

    def go(copy):
        copy.start()
        pending.append(copy)

    for q in range(2):
        for way in range(2):
            go(ring(way, 0, q))
    for q in range(2):
        go(to_twin(0, q))
    for hop in range(1, 4):
        for q in range(2):
            for way in range(2):
                ring_in(way, hop - 1, q).wait_recv()
                if hop < 3 or q == way:
                    go(ring(way, hop, q))
                go(to_twin(hop if way == 0 else NY - hop, q))
    for way in range(2):
        ring_in(way, 3, way).wait_recv()
        go(to_twin(4, way))
    own_a.wait()
    for back in (0, 1, 7, 2, 6, 3, 5, 4):
        for q in range(2):
            from_twin(back, q).wait_recv()

    def least(n):
        return (mode >= n).astype(jnp.int32)

    block = least(1) + least(2) + least(4) + least(6) + least(9)
    first = least(1) + least(2) + 2 * least(4) + 2 * least(6) + 3 * least(9)
    pair = jnp.minimum(mode - first, 2)
    row0 = pl.multiple_of(block * 128, 128)
    col0 = pl.multiple_of(pair * 256, 128)
    step = 256

    def gram_step(i, acc):
        k = pl.ds(pl.multiple_of(i * step, 128), step)
        return acc + dot(s_all[pl.ds(row0, 128), k], s_all[pl.ds(col0, 256), k], ((1,), (1,)))

    unit = lax.fori_loop(0, wide // step, gram_step, jnp.zeros((128, 256), jnp.float32))
    for t in range(32):
        r, h = 8 * (t // 2), 128 * (t % 2)
        g_part[t // 8, t % 8] = unit[r : r + 8, h : h + 128]

    def x_sum(part, landing, send, recv):
        out = [copy_to(part.at[(x + d) % NX], landing.at[d - 1], send.at[d - 1], recv.at[d - 1], at_x(d)) for d in range(1, NX)]

        def finish(spread):
            for c in out:
                c.wait_recv()
            spread[z] = (part[x] + landing[0] + landing[1] + landing[2]) * (1.0 / total)

        for c in out:
            go(c)
        return finish

    def z_sum(spread, send, recv):
        for d in range(1, NZ):
            go(copy_to(spread.at[z], spread.at[z], send.at[d - 1], recv.at[d - 1], at_z(d)))

        def finish(place):
            for d in range(1, NZ):
                ref = spread.at[(z + NZ - d) % NZ]
                copy_to(ref, ref, send.at[d - 1], recv.at[d - 1], at_z(d)).wait_recv()
            value = spread[0]
            for i in range(1, NZ):
                value = value + spread[i]
            place[core, y, x] = value

        return finish

    def y_spread(place, send, recv, count):
        def out(d):
            ref = place.at[core, y, x]
            return copy_to(ref, ref, send.at[d - 1], recv.at[d - 1], at_y(d))

        def start():
            for d in range(1, NY):
                out(d).start()

        def finish():
            for d in range(1, NY):
                def wait():
                    ref = place.at[core, (y + NY - d) % NY, x]
                    copy_to(ref, ref, send.at[d - 1], recv.at[d - 1], at_y(d)).wait_recv()
                if count < NY:
                    pl.when((y + NY - d) % NY < count)(wait)
                else:
                    wait()

        def sent():
            for d in range(1, NY):
                out(d).wait_send()

        if count < NY:
            pl.when(y < count)(start)
        else:
            start()
        return finish, sent

    def x_spread(place, send, recv, count):
        def ref(at):
            return place.at[core, pl.ds(0, count), at]

        for d in range(1, NX):
            go(copy_to(ref(x), ref(x), send.at[d - 1], recv.at[d - 1], at_x(d)))

        def finish():
            for d in range(1, NX):
                r = ref((x + NX - d) % NX)
                copy_to(r, r, send.at[d - 1], recv.at[d - 1], at_x(d)).wait_recv()

        return finish

    def twin_spread(place, send, recv, count):
        def ref(which):
            return place.at[which, pl.ds(0, count)]

        go(copy_to(ref(core), ref(core), send.at[0], recv.at[0], twin))

        def finish():
            copy_to(ref(1 - core), ref(1 - core), send.at[0], recv.at[0], twin).wait_recv()

        return finish

    g_x_done = x_sum(g_part, g_x, gx_send, gx_recv)

    def cross_step(i, acc):
        k = pl.ds(pl.multiple_of(i * step, 128), step)
        return acc + dot(a_own[:, k], s_all[:, k], ((1,), (1,)))

    crosst = lax.fori_loop(0, wide // step, cross_step, jnp.zeros((rows, s_all.shape[0]), jnp.float32))
    for t in range(36):
        r, h = 8 * (t // 6), 128 * (t % 6)
        c_part[t // 9, t % 9] = crosst[r : r + 8, h : h + 128]

    g_x_done(g_z)
    g_z_done = z_sum(g_z, gz_send, gz_recv)
    c_x_done = x_sum(c_part, c_x, cx_send, cx_recv)
    g_z_done(g_all)
    g_y_done, g_y_sent = y_spread(g_all, gy_send, gy_recv, UNITS // 2)
    c_x_done(c_z)
    c_z_done = z_sum(c_z, cz_send, cz_recv)
    g_y_done()
    g_s_done = x_spread(g_all, gg_send, gg_recv, UNITS // 2)
    c_z_done(c_all)
    c_y_done, c_y_sent = y_spread(c_all, cy_send, cy_recv, NY)
    g_s_done()
    g_t_done = twin_spread(g_all, gt_send, gt_recv, UNITS // 2)
    g_t_done()
    for u, (i, p) in enumerate(UNIT_PLACES):
        for t in range(32):
            r, h = i * 128 + 8 * (t // 2), p * 256 + 128 * (t % 2)
            z_ref[r : r + 8, h : h + 128] = g_all[u % 2, u // 2, t // 8, t % 8]
    c_y_done()
    c_s_done = x_spread(c_all, cg_send, cg_recv, NY)

    invert_lower(z_ref, d_ref, m_ref)

    c_s_done()
    c_t_done = twin_spread(c_all, ct_send, ct_recv, NY)
    lower = z_ref[pl.ds(pl.multiple_of(mode * rows, 8), rows), :]

    @pl.loop(0, wide // step)
    def _(i):
        k = pl.ds(pl.multiple_of(i * step, 128), step)
        ortho_ref[:, k] = dot(lower, s_all[:, k], ((1,), (0,)))

    c_t_done()
    for m in range(2 * NY):
        for t in range(36):
            r, h = m * rows + 8 * (t // 6), 128 * (t % 6)
            ct_ref[r : r + 8, h : h + 128] = c_all[m % 2, m // 2, t // 9, t % 9]
    half = dot(lower, ct_ref[...], ((1,), (1,)))
    proj_ref[...] = dot(half, z_ref[...], ((1,), (1,)))
    for c in pending:
        c.wait_send()
    pl.when(y < UNITS // 2)(g_y_sent)
    c_y_sent()


def per_device(subspace, applied):
    rows, wide = subspace.shape
    n = rows * lax.axis_size("modes")
    f32 = jnp.float32
    dma = pltpu.SemaphoreType.DMA
    exchange = lambda: [dma((NX - 1,))] * 2 + [dma((NZ - 1,))] * 2 + [dma((NY - 1,))] * 2 + [dma((NX - 1,))] * 2 + [dma((1,))] * 2
    return pl.pallas_call(
        kernel,
        out_shape=(
            jax.ShapeDtypeStruct((rows, wide), f32),
            jax.ShapeDtypeStruct((rows, n), f32),
        ),
        in_specs=[pl.BlockSpec(memory_space=pl.ANY)] * 2,
        out_specs=[pl.BlockSpec(memory_space=pltpu.VMEM)] * 2,
        scratch_shapes=[
            pltpu.VMEM((n, wide), f32),
            pltpu.VMEM((rows, wide), f32),
            pltpu.VMEM((NX, 8, 8, 128), f32),
            pltpu.VMEM((NX - 1, 8, 8, 128), f32),
            pltpu.VMEM((NZ, 8, 8, 128), f32),
            pltpu.VMEM((2, UNITS // 2 + 2, NX, 8, 8, 128), f32),
            pltpu.VMEM((NX, 9, 8, 128), f32),
            pltpu.VMEM((NX - 1, 9, 8, 128), f32),
            pltpu.VMEM((NZ, 9, 8, 128), f32),
            pltpu.VMEM((2, NY, NX, 9, 8, 128), f32),
            pltpu.VMEM((n, n), f32),
            pltpu.VMEM((n, n), f32),
            pltpu.VMEM((B, B), f32),
            pltpu.VMEM((B, B), f32),
            dma((2,)),
            dma((2, 4, 2)), dma((2, 4, 2)), dma((NY, 2)), dma((NY, 2)),
            *exchange(), *exchange(),
        ],
        compiler_params=pltpu.CompilerParams(
            collective_id=0, has_side_effects=True, vmem_limit_bytes=56 * 2**20
        ),
        name="cholesky_qr",
    )(subspace, applied)


def solution(mesh):
    return jax.shard_map(
        per_device,
        mesh=mesh,
        in_specs=(P("modes", "atoms"), P("modes", "atoms")),
        out_specs=(P("modes", "atoms"), P("modes", None)),
        check_vma=False,
    )
```

time: 220 us -> 141 us (0.64)
  Pallas kernels: 39.2 us -> 138 us
  waiting for transfers between devices: 97.9 us -> 0 us
  blocking collectives: 37.2 us -> 0 us
  matrix products: 27.2 us -> 0 us
  between operations: 14.2 us -> 0.65 us
    pallas_call x1, Pallas kernels: 39.2 us -> 138 us  [per_device(): pl.pallas_call(kernel, out_shape=(jax.ShapeDtypeStruct((rows, wide), f32)...]
    all_gather x2 -> x0, waiting for transfers between devices: 97.2 us -> none  [the longest x1 56.6 us: per_device(): full_modes = lax.all_gather(subspace, 'modes', axis=0, tiled=True)]
    all_to_all x2 -> x0, blocking collectives: 37.2 us -> none  [the longest x1 22 us: sum_at_owner(): tiles = lax.all_to_all(in_blocks(value, dim, count), axis, 0, 0, tiled=True)]
    dot_general x5 -> x0, matrix products: 27.2 us -> none  [the longest x2 17.4 us: contract_cols(): lax.dot_general(left, right, (((1,), (1,)), ((), ())), precision=lax.Prec...]
    slice x2 -> x0, local copies, waits for them, and re-layouts: 2.71 us -> none  [the longest x1 1.97 us: sent_together(): gathered.append(lax.slice_in_dim(out, at, at + a.shape[along], axis=along))]
    unnamed x8 -> x4, local copies, waits for them, and re-layouts: 0.02 us -> 2.47 us
  transfers between devices with their start and end apart: 2 -> 0, of which waited for: 2 -> 0; matrix products, arithmetic and copies ran while one was open for 0% -> 0% of each run, Pallas kernels for 0% -> 0%
where the time goes in v1:
time: 141 us
  Pallas kernels  138 us (98%)
  local copies, waits for them, and re-layouts  2.47 us (2%)
    pallas_call x1, Pallas kernels, per_device(): pl.pallas_call(kernel, out_shape=(jax.ShapeDtypeStruct((rows, wide), f32)...  138 us

profile of v1, /device:TPU:1, one launch (start us, length us, event | category | flops | bytes accessed | tf_op | source)
XLA Modules:
  0.0 140.7 jit_solution(10964969067793004572)
XLA Ops:
  0.6 137.6 %cholesky_qr.1 = (f32[48,2048]{1,0:T(8,128)}, f32[48,768]{1,0:T(8,128)}) custom-call(f32[48,2048]{1,0:T(8,128)} %s_hbm.1, f32[48,2048]{1,0:T(8,128)} %a_hbm.1), custom_call_target="tpu_custom_call" | custom-call | tf_op jit(solution)/shard_map/cholesky_qr/pallas_call | solution.py:375
  138.2 0.0 copy-start
  138.2 1.8 %copy.6 = f32[48,2048]{1,0:T(8,128)} copy(f32[48,2048]{1,0:T(8,128)} %get-tuple-element.4) | data formatting | bytes 786432
  140.0 0.0 copy-done
  140.0 0.7 copy.7
Async XLA Ops:
  138.2 1.8 %copy-start = (f32[48,768]{1,0:T(8,128)S(1)}, f32[48,768]{1,0:T(8,128)}, u32[]{:S(2)}) copy-start(f32[48,768]{1,0:T(8,128)} %get-tuple-element.5) | copy-start | bytes 442372
